TPU v7x, 32 devices: a whole 2x2x4 slice. The times are simulated.
32 devices in a mesh: cfg: 2 (over x), seq: 16 (over z, y, core).
Axes of the slice: x: 2, y: 2, z: 4, core: 2. Of those that a mesh axis runs over, the one named last changes fastest.
Arguments:
- hidden: bfloat16 [2, 2048, 1920], P('cfg', 'seq'), may hold values from -6 to 6
- modulation: float32 [6, 1920], replicated, may hold values from -3 to 3
- w_qkv: bfloat16 [3, 1920, 1024], replicated, may hold values from -0.125 to 0.125
- q_gain: float32 [64], replicated, may hold values from 1 to 13, as said below
- k_gain: float32 [64], replicated, may hold values from 1 to 13, as said below
- w_out: bfloat16 [1024, 1920], replicated, may hold values from -0.1875 to 0.1875
- text_count: int32 [2], P('cfg'), may hold values from 1 to 226
- block_order: int32 [16], P('seq'), may hold values from 0 to 15, each once
Outputs:
- guided: float32 [2048, 1920], P('seq', 'cfg')
Inputs may be any that keep to these rules, and one draw needn't show every extreme that they name: text_count[b] is how many of the 226 text positions of branch b (0 conditional, 1 unconditional) hold prompt tokens; keys at the other text positions are masked. Seq index j holds positions block_order[j] * 128 to block_order[j] * 128 + 127; every block appears once. `q_gain`: one gain for each of the 64 entries of a head, shared by all heads. `k_gain`: one gain for each of the 64 entries of a head, shared by all heads.
All inputs are finite; a program needn't handle non-finite values.
Results may differ from a plain program's by a relative error of at most 0.015.
The roundings to bfloat16 on the way count: a program that leaves them out, or rounds other values in their place, can miss the bound.
Values may be sent and summed in bfloat16 or wider, within the bound.
A program may use at most 256 MiB of HBM per device.

v0:
```python
import functools

import jax
import jax.numpy as jnp
from jax import lax
from jax.experimental import pallas as pl
from jax.experimental.pallas import tpu as pltpu
from jax.sharding import PartitionSpec as P

HEAD = 64
HEADS = 16
TXT = 226


GUIDANCE = 6.0
EPSILON = 1e-05
MASKED = -1000000000.0


def swapped(block, axis, apart):
    count = lax.axis_size(axis)
    route = []
    for low in range(count):
        high = low | 1 << apart
        if high != low and high < count:
            route += [(low, high), (high, low)]
    return lax.ppermute(block, axis, route)


def layer_normal(values_in):
    average = jnp.mean(values_in, axis=-1, keepdims=True)
    centred = values_in - average
    spread = jnp.mean(centred * centred, axis=-1, keepdims=True)
    return centred * lax.rsqrt(spread + EPSILON)


def modulated(states, is_text, modulation):
    normed = layer_normal(states.astype(jnp.float32))
    shift = jnp.where(is_text[:, None], modulation[3][None, :], modulation[0][None, :])
    scale = jnp.where(is_text[:, None], modulation[4][None, :], modulation[1][None, :])
    return (normed * (1.0 + scale) + shift).astype(jnp.bfloat16)


def head_normal(projected, gain):
    rows = projected.shape[0]
    heads_view = projected.reshape(rows, HEADS, HEAD)
    return (layer_normal(heads_view) * gain).reshape(rows, HEADS * HEAD).astype(jnp.bfloat16)


def projections(states, is_text, modulation, w_qkv, q_gain, k_gain):
    modded = modulated(states, is_text, modulation)
    query = head_normal(jnp.dot(modded, w_qkv[0], preferred_element_type=jnp.float32), q_gain)
    keys = head_normal(jnp.dot(modded, w_qkv[1], preferred_element_type=jnp.float32), k_gain)
    values = jnp.dot(modded, w_qkv[2], preferred_element_type=jnp.float32).astype(jnp.bfloat16)
    return (query, keys, values)


def fold_block(query_heads, carry, piece):
    highest, total, numer = carry
    keys_piece, values_piece, bias_piece = piece
    count = keys_piece.shape[0]
    key_heads = keys_piece.reshape(count, HEADS, HEAD)
    value_heads = values_piece.reshape(count, HEADS, HEAD)
    scores = jnp.einsum("qhd,khd->hqk", query_heads, key_heads, preferred_element_type=jnp.float32)
    scores = scores * HEAD ** (-0.5) + bias_piece.astype(jnp.float32)[None, None, :]
    new_high = jnp.maximum(highest, jnp.max(scores, axis=-1))
    expo = jnp.exp(scores - new_high[:, :, None])
    rescale = jnp.exp(highest - new_high)
    total = jnp.sum(expo, axis=-1)
    numer = numer * rescale.T[:, :, None] + jnp.einsum(
        "hqk,khd->qhd", expo.astype(jnp.bfloat16), value_heads, preferred_element_type=jnp.float32
    )
    return (new_high, total, numer)


def shards(hidden, modulation, w_qkv, q_gain, k_gain, w_out, text_count, block_order):
    states = hidden[0]
    tok_rows = states.shape[0]
    within = jnp.arange(tok_rows, dtype=jnp.int32)
    position = block_order[0] * tok_rows + within
    is_text = position < TXT
    keep = jnp.logical_or(position >= TXT, position < text_count[0])
    key_bias = jnp.where(keep, 0.0, MASKED).astype(jnp.bfloat16)
    query, keys, values = projections(states, is_text, modulation, w_qkv, q_gain, k_gain)
    query_heads = query.reshape(tok_rows, HEADS, HEAD)
    start_state = (
        jnp.full((HEADS, tok_rows), -1e30, jnp.float32),
        jnp.zeros((HEADS, tok_rows), jnp.float32),
        jnp.zeros((tok_rows, HEADS, HEAD), jnp.float32),
    )
    carry = fold_block(
        query_heads,
        start_state,
        (
            lax.all_gather(keys, "seq", axis=0, tiled=True),
            lax.all_gather(values, "seq", axis=0, tiled=True),
            lax.all_gather(key_bias, "seq", axis=0, tiled=True),
        ),
    )
    highest, total, numer = carry
    attended = (numer / total.T[:, :, None]).reshape(tok_rows, HEADS * HEAD).astype(jnp.bfloat16)
    gate = jnp.where(is_text[:, None], modulation[5][None, :], modulation[2][None, :])
    cfg_index = lax.axis_index("cfg")
    half_width = w_out.shape[1] // 2
    w_half = lax.dynamic_slice_in_dim(w_out, cfg_index * half_width, half_width, 1)
    gate_half = lax.dynamic_slice_in_dim(gate, cfg_index * half_width, half_width, 1)
    partner = swapped(attended, "cfg", 0)
    own_update = gate_half * jnp.dot(attended, w_half, preferred_element_type=jnp.float32)
    other_update = gate_half * jnp.dot(partner, w_half, preferred_element_type=jnp.float32)
    is_first = cfg_index == 0
    cond = jnp.where(is_first, own_update, other_update)
    uncond = jnp.where(is_first, other_update, own_update)
    return uncond + GUIDANCE * (cond - uncond)


LANES = 128
GROUPS = 4
MESH = pl.DeviceIdType.MESH


def flip(bit, other):
    return lax.rem(bit + other, 2)


def pair_normal(x, low):
    def halves(y):
        first = jnp.sum(jnp.where(low, y, 0.0), axis=-1, keepdims=True)
        second = jnp.sum(jnp.where(low, 0.0, y), axis=-1, keepdims=True)
        return jnp.where(low, first, second) * (1.0 / HEAD)

    centred = x - halves(x)
    return centred * lax.rsqrt(halves(centred * centred) + EPSILON)


def turned(x):
    return pltpu.roll(x, HEAD, 1)


def fused(n, count_ref, block_ref, hidden_ref, mod_ref, w_ref, qg_ref, kg_ref, wo_ref, out_ref,
          w_buf, wo_buf, modded, kv_out, kv_in, q_out, q_in, bias_out, bias_in, bias_row,
          att_out, att_in, att_far, stacked,
          w_sem, wo_sem, kv_s, kv_r, q_s, q_r, b_s, b_r, a_s, a_r, f_s, f_r):
    me = lax.axis_index("seq")
    cfg = lax.axis_index("cfg")
    rows, width = hidden_ref.shape
    half_rows = rows // 2
    half = width // 2
    wide = wo_buf.shape[1]
    cols = w_buf.shape[3]
    heads_here = cols // HEAD
    plane = lax.div(me, GROUPS)
    plane_high, plane_low = lax.div(plane, 2), lax.rem(plane, 2)

    def group(i):
        high = 1 - lax.div(i, 2)
        lowbit = flip(lax.div(i, 2), lax.rem(i, 2))
        return 2 * flip(plane_high, high) + flip(plane_low, lowbit)

    def weight(kind, i):
        start = pl.multiple_of(group(i) * cols, cols)
        return pltpu.make_async_copy(
            w_ref.at[kind, :, pl.ds(start, cols)], w_buf.at[kind, i], w_sem.at[kind, i])

    column = pl.multiple_of(cfg * (width - wide), LANES)
    out_weight = pltpu.make_async_copy(wo_ref.at[:, pl.ds(column, wide)], wo_buf, wo_sem)

    barrier = pltpu.get_barrier_semaphore()
    for j in range(1, n):
        pl.semaphore_signal(barrier, inc=1, device_id={"seq": lax.rem(me + j, n)}, device_id_type=MESH)
    pl.semaphore_signal(barrier, inc=1, device_id={"cfg": 1 - cfg}, device_id_type=MESH)
    for i in range(GROUPS):
        weight(1, i).start()
        weight(2, i).start()
    for i in range(GROUPS):
        weight(0, i).start()
    out_weight.start()

    def send(src, dst, to, s_sem, r_sem):
        @pl.when(to != me)
        def _():
            pltpu.make_async_remote_copy(
                src_ref=src.at[to], dst_ref=dst.at[me], send_sem=s_sem.at[to], recv_sem=r_sem.at[me],
                device_id={"seq": to}, device_id_type=MESH).start()

        @pl.when(to == me)
        def _():
            pltpu.make_async_copy(src.at[to], dst.at[me], r_sem.at[me]).start()

    def arrived(dst, source, r_sem):
        pltpu.make_async_copy(dst.at[source], dst.at[source], r_sem.at[source]).wait()

    def sent(src, to, s_sem):
        @pl.when(to != me)
        def _():
            pltpu.make_async_copy(src.at[to], src.at[to], s_sem.at[to]).wait()

    block = block_ref[0]
    count = count_ref[0]
    across = block * rows + lax.broadcasted_iota(jnp.int32, (1, rows), 1)
    keep = jnp.logical_or(across >= TXT, across < count)
    bias_out[0:n] = jnp.broadcast_to(jnp.where(keep, 0.0, MASKED)[None], (n, 1, rows)).astype(jnp.bfloat16).astype(jnp.float32)

    mod = mod_ref[...]
    down = block * rows + lax.broadcasted_iota(jnp.int32, (rows, 1), 0)
    is_text = down < TXT
    normed = layer_normal(hidden_ref[...].astype(jnp.float32))
    shift = jnp.where(is_text, mod[3:4, :], mod[0:1, :])
    scale = jnp.where(is_text, mod[4:5, :], mod[1:2, :])
    modded[...] = (normed * (1.0 + scale) + shift).astype(jnp.bfloat16)

    low = lax.broadcasted_iota(jnp.int32, (1, LANES), 1) < HEAD
    pl.semaphore_wait(barrier, n)

    def send_bias(j, carry):
        send(bias_out, bias_in, j, b_s, b_r)
        return carry

    lax.fori_loop(0, n, send_bias, 0)

    k_gain = kg_ref[...]
    q_gain = qg_ref[...] * HEAD ** (-0.5)

    def project_kv(i, carry):
        weight(1, i).wait()
        weight(2, i).wait()
        first = group(i) * heads_here
        x = modded[...]
        k_all = jnp.dot(x, w_buf[1, i], preferred_element_type=jnp.float32)
        v_all = jnp.dot(x, w_buf[2, i], preferred_element_type=jnp.float32)
        for p in range(heads_here // 2):
            k = pair_normal(k_all[:, p * LANES:(p + 1) * LANES], low) * k_gain
            v = v_all[:, p * LANES:(p + 1) * LANES]
            kv_out[first + 2 * p] = jnp.where(low, k, turned(v)).astype(jnp.bfloat16)
            kv_out[first + 2 * p + 1] = jnp.where(low, turned(k), v).astype(jnp.bfloat16)
        for h in range(heads_here):
            send(kv_out, kv_in, first + h, kv_s, kv_r)
        return carry

    lax.fori_loop(0, GROUPS, project_kv, 0)

    def project_q(i, carry):
        weight(0, i).wait()
        first = group(i) * heads_here
        q_all = jnp.dot(modded[...], w_buf[0, i], preferred_element_type=jnp.float32)
        for p in range(heads_here // 2):
            q = pair_normal(q_all[:, p * LANES:(p + 1) * LANES], low) * q_gain
            top, bottom = q[:half_rows], q[half_rows:]
            q_out[first + 2 * p] = jnp.where(low, top, turned(bottom)).astype(jnp.bfloat16)
            q_out[first + 2 * p + 1] = jnp.where(low, turned(top), bottom).astype(jnp.bfloat16)
        for h in range(heads_here):
            send(q_out, q_in, first + h, q_s, q_r)
        return carry

    lax.fori_loop(0, GROUPS, project_q, 0)

    for j in range(n):
        arrived(bias_in, j, b_r)
    for j in range(n):
        bias_row[:, j * rows:(j + 1) * rows] = jnp.broadcast_to(bias_in[j], (8, rows))

    def wait_kv(j, carry):
        arrived(kv_in, j, kv_r)
        return carry

    lax.fori_loop(0, n, wait_kv, 0)

    chip = lax.div(me, 2)

    def pair_of(k):
        c0, c1, c2 = lax.rem(chip, 2), lax.rem(lax.div(chip, 2), 2), lax.div(chip, 4)
        k0, k1, k2 = lax.rem(k, 2), lax.rem(lax.div(k, 2), 2), lax.div(k, 4)
        return 4 * flip(c2, k2) + 2 * flip(c1, k1) + flip(c0, k0)

    def forward(k):
        for i in range(2):
            h = 2 * pair_of(k) + i
            arrived(att_in, h, a_r)
            pltpu.make_async_remote_copy(
                src_ref=att_in.at[h], dst_ref=att_far.at[h], send_sem=f_s.at[h], recv_sem=f_r.at[h],
                device_id={"cfg": 1 - cfg}, device_id_type=MESH).start()

    def attend(k, carry):
        base = 2 * pair_of(k)
        parts = []
        for i in range(2):
            arrived(q_in, base + i, q_r)
            folded = q_in[base + i].astype(jnp.float32)
            parts += [jnp.where(low, folded, 0.0), jnp.where(low, turned(folded), 0.0)]
        query = jnp.concatenate(parts, axis=0).astype(jnp.bfloat16)
        keys = kv_in[...].reshape(n * rows, LANES)
        scores = lax.dot_general(query, keys, (((1,), (1,)), ((), ())), preferred_element_type=jnp.float32)
        scores = scores + bias_row[0:1, :]
        expo = jnp.exp(scores - jnp.max(scores, axis=-1, keepdims=True))
        total = jnp.sum(expo, axis=-1, keepdims=True)
        numer = jnp.dot(expo.astype(jnp.bfloat16), keys, preferred_element_type=jnp.float32)
        result = numer / total
        for i in range(2):
            top = result[i * rows:i * rows + half_rows]
            bottom = result[i * rows + half_rows:(i + 1) * rows]
            att_out[base + i] = jnp.where(low, turned(top), bottom).astype(jnp.bfloat16)
            send(att_out, att_in, base + i, a_s, a_r)

        @pl.when(k >= 2)
        def _():
            forward(k - 2)

        return carry

    steps = n // 2
    lax.fori_loop(0, steps, attend, 0)
    forward(steps - 2)
    forward(steps - 1)
    out_weight.wait()

    def assemble(source, at):
        for p in range(n // 2):
            a = source[2 * p].astype(jnp.float32)
            b = source[2 * p + 1].astype(jnp.float32)
            span = slice(p * LANES, (p + 1) * LANES)
            stacked[at:at + half_rows, span] = jnp.where(low, a, turned(b)).astype(jnp.bfloat16)
            stacked[at + half_rows:at + rows, span] = jnp.where(low, turned(a), b).astype(jnp.bfloat16)

    assemble(att_in, 0)
    for h in range(n):
        arrived(att_far, h, f_r)
    assemble(att_far, rows)
    both = jnp.dot(stacked[...], wo_buf[...], preferred_element_type=jnp.float32)
    is_first = cfg == 0
    gate_text = jnp.where(is_first, mod[5:6, :wide], mod[5:6, width - wide:])
    gate_video = jnp.where(is_first, mod[2:3, :wide], mod[2:3, width - wide:])
    gate = jnp.where(is_text, gate_text, gate_video)
    own, other = gate * both[:rows], gate * both[rows:]
    cond = jnp.where(is_first, own, other)
    uncond = jnp.where(is_first, other, own)
    guided = uncond + GUIDANCE * (cond - uncond)
    excess = wide - half
    guided = jnp.where(is_first, guided, pltpu.roll(guided, half, 1)) if excess else guided
    out_ref[...] = guided[:, :half]

    def finish(j, carry):
        sent(bias_out, j, b_s)
        sent(kv_out, j, kv_s)
        sent(q_out, j, q_s)
        sent(att_out, j, a_s)
        pltpu.make_async_copy(att_in.at[j], att_in.at[j], f_s.at[j]).wait()
        return carry

    lax.fori_loop(0, n, finish, 0)


def whole_kernel(hidden, modulation, w_qkv, q_gain, k_gain, w_out, text_count, block_order):
    n = lax.axis_size("seq")
    states = hidden[0]
    rows, width = states.shape
    features = w_out.shape[0]
    cols = features // GROUPS
    half = width // 2
    wide = -(-half // LANES) * LANES
    bf, f32 = jnp.bfloat16, jnp.float32
    vmem = pl.BlockSpec(memory_space=pltpu.VMEM)
    smem = pl.BlockSpec(memory_space=pltpu.SMEM)
    hbm = pl.BlockSpec(memory_space=pl.ANY)
    dma = pltpu.SemaphoreType.DMA
    double = lambda gain: jnp.concatenate([gain, gain])[None, :]
    return pl.pallas_call(
        functools.partial(fused, n),
        out_shape=jax.ShapeDtypeStruct((rows, half), f32),
        in_specs=[smem, smem, vmem, vmem, hbm, vmem, vmem, hbm],
        out_specs=vmem,
        scratch_shapes=[
            pltpu.VMEM((3, GROUPS, width, cols), bf),
            pltpu.VMEM((features, wide), bf),
            pltpu.VMEM((rows, width), bf),
            pltpu.VMEM((n, rows, LANES), bf),
            pltpu.VMEM((n, rows, LANES), bf),
            pltpu.VMEM((n, rows // 2, LANES), bf),
            pltpu.VMEM((n, rows // 2, LANES), bf),
            pltpu.VMEM((n + 8, 1, rows), f32),
            pltpu.VMEM((n + 8, 1, rows), f32),
            pltpu.VMEM((8, n * rows), f32),
            pltpu.VMEM((n, rows // 2, LANES), bf),
            pltpu.VMEM((n, rows // 2, LANES), bf),
            pltpu.VMEM((n, rows // 2, LANES), bf),
            pltpu.VMEM((2 * rows, features), bf),
            dma((3, GROUPS)),
            dma,
        ] + [dma((n,))] * 10,
        compiler_params=pltpu.CompilerParams(
            collective_id=0, has_side_effects=True, vmem_limit_bytes=60 * 1024 * 1024),
    )(text_count, block_order, states, modulation, w_qkv, double(q_gain), double(k_gain), w_out)


def solution(mesh):
    in_specs = (P("cfg", "seq", None), P(), P(), P(), P(), P(), P("cfg"), P("seq"))
    out_specs = P("seq", "cfg")
    one_head_each = mesh.shape["seq"] == HEADS and mesh.shape["cfg"] == 2
    body = whole_kernel if one_head_each else shards
    return jax.shard_map(body, mesh=mesh, in_specs=in_specs, out_specs=out_specs, check_vma=False)
```

profile of v0, /device:TPU:0, one launch (start us, length us, event | category | flops | bytes accessed | tf_op | source)
XLA Modules:
  0.0 50.0 jit_solution(15077264683599628902)
XLA Ops:
  1.3 1.3 %maximum_bitcast_fusion = (f32[1,128]{1,0:T(1,128)}, f32[1,128]{1,0:T(1,128)}) fusion(f32[64]{0:T(128)} %param.11, f32[64]{0:T(128)} %param.12), kind=kLoop, calls=%fused_computation | loop fusion | flops 256 | bytes 1536 | tf_op jit(solution)/shard_map/broadcast_in_dim | solution.py:364
  2.6 45.3 %shard_map.82 = f32[128,960]{1,0:T(8,128)} custom-call(s32[1]{0:T(128)S(6)} %copy.10.count_ref, s32[1]{0:T(128)S(6)} %copy.11.block_ref, bf16[128,1920]{1,0:T(8,128)(2,1)} %bitcast.5, f32[6,1920]{1,0:T(8,128)} %mod_ref.1, bf16[3,1920,1024]{2,1,0:T(8,128)(2,1)} %w_ref.1, f32[1,128]{1,0:T(1,128)} %get-tuple-element.5.qg_ref, ...), custom_call_target="tpu_custom_call" | custom-call | tf_op jit(solution)/shard_map/pallas_call | solution.py:365
  47.9 2.0 %copy.9 = f32[128,960]{0,1:T(8,128)} copy(f32[128,960]{1,0:T(8,128)} %shard_map.82) | data formatting | bytes 983040 | tf_op jit(solution)/shard_map/pallas_call | solution.py:365
where the time goes:
time: 50.2 us; the launch traced here: 50 us
  Pallas kernels  45.3 us (90%)
  local copies, waits for them, and re-layouts  2.02 us (4%)
  other arithmetic  1.32 us (3%)
  between operations  1.31 us (3%)
    pallas_call x1, Pallas kernels, whole_kernel(): pl.pallas_call(functools.partial(fused, n), out_shape=jax.ShapeDtypeStruc...  45.3 us
    pallas_call x1, local copies, waits for them, and re-layouts, whole_kernel(): pl.pallas_call(functools.partial(fused, n), out_shape=jax.ShapeDtypeStruc...  2.02 us
    broadcast_in_dim x1, other arithmetic, whole_kernel(): double = lambda gain: jnp.concatenate([gain, gain])[None, :]  1.32 us

commit v1 on v0

v1 whole, which is shorter than its diff:
```python
import functools

import jax
import jax.numpy as jnp
from jax import lax
from jax.experimental import pallas as pl
from jax.experimental.pallas import tpu as pltpu
from jax.sharding import PartitionSpec as P

HEAD = 64
HEADS = 16
TXT = 226


GUIDANCE = 6.0
EPSILON = 1e-05
MASKED = -1000000000.0


def swapped(block, axis, apart):
    count = lax.axis_size(axis)
    route = []
    for low in range(count):
        high = low | 1 << apart
        if high != low and high < count:
            route += [(low, high), (high, low)]
    return lax.ppermute(block, axis, route)


def layer_normal(values_in):
    average = jnp.mean(values_in, axis=-1, keepdims=True)
    centred = values_in - average
    spread = jnp.mean(centred * centred, axis=-1, keepdims=True)
    return centred * lax.rsqrt(spread + EPSILON)


def modulated(states, is_text, modulation):
    normed = layer_normal(states.astype(jnp.float32))
    shift = jnp.where(is_text[:, None], modulation[3][None, :], modulation[0][None, :])
    scale = jnp.where(is_text[:, None], modulation[4][None, :], modulation[1][None, :])
    return (normed * (1.0 + scale) + shift).astype(jnp.bfloat16)


def head_normal(projected, gain):
    rows = projected.shape[0]
    heads_view = projected.reshape(rows, HEADS, HEAD)
    return (layer_normal(heads_view) * gain).reshape(rows, HEADS * HEAD).astype(jnp.bfloat16)


def projections(states, is_text, modulation, w_qkv, q_gain, k_gain):
    modded = modulated(states, is_text, modulation)
    query = head_normal(jnp.dot(modded, w_qkv[0], preferred_element_type=jnp.float32), q_gain)
    keys = head_normal(jnp.dot(modded, w_qkv[1], preferred_element_type=jnp.float32), k_gain)
    values = jnp.dot(modded, w_qkv[2], preferred_element_type=jnp.float32).astype(jnp.bfloat16)
    return (query, keys, values)


def fold_block(query_heads, carry, piece):
    highest, total, numer = carry
    keys_piece, values_piece, bias_piece = piece
    count = keys_piece.shape[0]
    key_heads = keys_piece.reshape(count, HEADS, HEAD)
    value_heads = values_piece.reshape(count, HEADS, HEAD)
    scores = jnp.einsum("qhd,khd->hqk", query_heads, key_heads, preferred_element_type=jnp.float32)
    scores = scores * HEAD ** (-0.5) + bias_piece.astype(jnp.float32)[None, None, :]
    new_high = jnp.maximum(highest, jnp.max(scores, axis=-1))
    expo = jnp.exp(scores - new_high[:, :, None])
    rescale = jnp.exp(highest - new_high)
    total = jnp.sum(expo, axis=-1)
    numer = numer * rescale.T[:, :, None] + jnp.einsum(
        "hqk,khd->qhd", expo.astype(jnp.bfloat16), value_heads, preferred_element_type=jnp.float32
    )
    return (new_high, total, numer)


def shards(hidden, modulation, w_qkv, q_gain, k_gain, w_out, text_count, block_order):
    states = hidden[0]
    tok_rows = states.shape[0]
    within = jnp.arange(tok_rows, dtype=jnp.int32)
    position = block_order[0] * tok_rows + within
    is_text = position < TXT
    keep = jnp.logical_or(position >= TXT, position < text_count[0])
    key_bias = jnp.where(keep, 0.0, MASKED).astype(jnp.bfloat16)
    query, keys, values = projections(states, is_text, modulation, w_qkv, q_gain, k_gain)
    query_heads = query.reshape(tok_rows, HEADS, HEAD)
    start_state = (
        jnp.full((HEADS, tok_rows), -1e30, jnp.float32),
        jnp.zeros((HEADS, tok_rows), jnp.float32),
        jnp.zeros((tok_rows, HEADS, HEAD), jnp.float32),
    )
    carry = fold_block(
        query_heads,
        start_state,
        (
            lax.all_gather(keys, "seq", axis=0, tiled=True),
            lax.all_gather(values, "seq", axis=0, tiled=True),
            lax.all_gather(key_bias, "seq", axis=0, tiled=True),
        ),
    )
    highest, total, numer = carry
    attended = (numer / total.T[:, :, None]).reshape(tok_rows, HEADS * HEAD).astype(jnp.bfloat16)
    gate = jnp.where(is_text[:, None], modulation[5][None, :], modulation[2][None, :])
    cfg_index = lax.axis_index("cfg")
    half_width = w_out.shape[1] // 2
    w_half = lax.dynamic_slice_in_dim(w_out, cfg_index * half_width, half_width, 1)
    gate_half = lax.dynamic_slice_in_dim(gate, cfg_index * half_width, half_width, 1)
    partner = swapped(attended, "cfg", 0)
    own_update = gate_half * jnp.dot(attended, w_half, preferred_element_type=jnp.float32)
    other_update = gate_half * jnp.dot(partner, w_half, preferred_element_type=jnp.float32)
    is_first = cfg_index == 0
    cond = jnp.where(is_first, own_update, other_update)
    uncond = jnp.where(is_first, other_update, own_update)
    return uncond + GUIDANCE * (cond - uncond)


LANES = 128
GROUPS = 4
MESH = pl.DeviceIdType.MESH


def flip(bit, other):
    return lax.rem(bit + other, 2)


def column_normal(x):
    centred = x - jnp.mean(x, axis=0, keepdims=True)
    spread = jnp.mean(centred * centred, axis=0, keepdims=True)
    return centred * lax.rsqrt(spread + EPSILON)


def fused(n, count_ref, block_ref, hidden_ref, mod_ref, w_ref, qg_ref, kg_ref, wo_ref, out_ref,
          count_v, block_v, hidden_v, mod_v, qg_v, kg_v, w_buf, wo_buf, wo_turned, gate, modded,
          kv_out, kv_in, q_out, q_in, place_out, place_in, keys, values,
          att_own, att_far, mixed, att_in,
          in_sem, w_sem, wo_sem, kv_s, kv_r, q_s, q_r, p_s, p_r, x_s, x_r, a_s, a_r):
    me = lax.axis_index("seq")
    cfg = lax.axis_index("cfg")
    rows, width = hidden_ref.shape
    half = width // 2
    wide = wo_buf.shape[1]
    excess = wide - half
    cols = w_buf.shape[3]
    heads_here = cols // HEAD
    steps = n // 2
    span = n * rows // 2
    bf, f32 = jnp.bfloat16, jnp.float32
    plane = lax.div(me, GROUPS)
    plane_high, plane_low = lax.div(plane, 2), lax.rem(plane, 2)
    side, core = lax.rem(lax.div(me, 2), 2), lax.rem(me, 2)

    barrier = pltpu.get_barrier_semaphore()
    for j in range(1, n):
        pl.semaphore_signal(barrier, inc=1, device_id={"seq": lax.rem(me + j, n)}, device_id_type=MESH)
    pl.semaphore_signal(barrier, inc=1, device_id={"cfg": 1 - cfg}, device_id_type=MESH)

    def group(i):
        high = 1 - lax.div(i, 2)
        lowbit = flip(lax.div(i, 2), lax.rem(i, 2))
        return 2 * flip(plane_high, high) + flip(plane_low, lowbit)

    def member(first, h):
        return first + 2 * flip(side, h // 2) + flip(core, h % 2)

    def weight(kind, i):
        start = pl.multiple_of(group(i) * cols, cols)
        return pltpu.make_async_copy(
            w_ref.at[kind, :, pl.ds(start, cols)], w_buf.at[kind, i], w_sem.at[kind, i])

    column = pl.multiple_of(cfg * (width - wide), LANES)
    out_weight = pltpu.make_async_copy(wo_ref.at[:, pl.ds(column, wide)], wo_buf, wo_sem)
    inputs = [pltpu.make_async_copy(a, b, in_sem.at[i]) for i, (a, b) in enumerate([
        (hidden_ref, hidden_v), (mod_ref, mod_v), (block_ref, block_v), (count_ref, count_v),
        (kg_ref, kg_v), (qg_ref, qg_v)])]
    for copy in inputs:
        copy.start()
    weight(1, 0).start()
    weight(2, 0).start()

    def send(src, dst, to, s_sem, r_sem):
        @pl.when(to != me)
        def _():
            pltpu.make_async_remote_copy(
                src_ref=src.at[to], dst_ref=dst.at[me], send_sem=s_sem, recv_sem=r_sem,
                device_id={"seq": to}, device_id_type=MESH).start()

        @pl.when(to == me)
        def _():
            dst[me] = src[to]

    def landed(ref, count, sem):
        part = ref.at[pl.ds(0, count)]
        pltpu.make_async_copy(part, part, sem).wait()

    for copy in inputs:
        copy.wait()
    block = block_v[...]
    count = count_v[...]
    mod = mod_v[...]
    down = block * rows + lax.broadcasted_iota(jnp.int32, (rows, 1), 0)
    is_text = down < TXT
    normed = layer_normal(hidden_v[...].astype(f32))
    shift = jnp.where(is_text, mod[3:4, :], mod[0:1, :])
    scale = jnp.where(is_text, mod[4:5, :], mod[1:2, :])
    modded[...] = (normed * (1.0 + scale) + shift).astype(bf)

    for i in range(1, GROUPS):
        weight(1, i).start()
        weight(2, i).start()
    for i in range(GROUPS):
        weight(0, i).start()
    out_weight.start()

    def down_lanes(gain_row):
        both = jnp.concatenate([gain_row, gain_row], axis=1)
        return jnp.broadcast_to(both, (LANES, LANES)).T[:HEAD]

    k_gain = down_lanes(kg_v[...])
    q_gain = down_lanes(qg_v[...]) * HEAD ** (-0.5)
    place_out[0] = jnp.broadcast_to(block, (1, LANES))
    place_in[me] = jnp.broadcast_to(block, (1, LANES))

    def project_kv(i):
        weight(1, i).wait()
        weight(2, i).wait()
        first = group(i) * heads_here
        x = modded[...]
        k_all = jnp.dot(x, w_buf[1, i], preferred_element_type=f32).T
        v_all = jnp.dot(x, w_buf[2, i], preferred_element_type=f32).T
        for h in range(heads_here):
            part = slice(h * HEAD, (h + 1) * HEAD)
            kv_out[first + h, :HEAD] = (column_normal(k_all[part]) * k_gain).astype(bf)
            kv_out[first + h, HEAD:] = v_all[part].astype(bf)

    def send_kv(i):
        first = group(i) * heads_here
        for h in range(heads_here):
            send(kv_out, kv_in, member(first, h), kv_s, kv_r)

    project_kv(0)
    pl.semaphore_wait(barrier, n)
    send_kv(0)
    for j in range(1, n):
        pltpu.make_async_remote_copy(
            src_ref=place_out.at[0], dst_ref=place_in.at[me], send_sem=p_s, recv_sem=p_r,
            device_id={"seq": lax.rem(me + j, n)}, device_id_type=MESH).start()

    def rest_kv(i, carry):
        project_kv(i)
        send_kv(i)
        return carry

    lax.fori_loop(1, GROUPS, rest_kv, 0)

    def project_q(i, carry):
        weight(0, i).wait()
        first = group(i) * heads_here
        q_all = jnp.dot(modded[...], w_buf[0, i], preferred_element_type=f32).T
        for h in range(heads_here):
            part = slice(h * HEAD, (h + 1) * HEAD)
            q_out[first + h] = (column_normal(q_all[part]) * q_gain).astype(bf)
        for h in range(heads_here):
            send(q_out, q_in, member(first, h), q_s, q_r.at[me])
        return carry

    lax.fori_loop(0, GROUPS, project_q, 0)

    out_weight.wait()

    def put(target, turned, c):
        @pl.when(cfg == 0)
        def _():
            low, high = c * LANES, min((c + 1) * LANES, half)
            target[low:high] = turned[:high - low]

        @pl.when(cfg != 0)
        def _():
            low, high = max(c * LANES - excess, 0), (c + 1) * LANES - excess
            target[low:high] = turned[LANES - (high - low):]

    gate_text = jnp.where(cfg == 0, mod_v[5:6, :wide], mod_v[5:6, width - wide:])
    gate_video = jnp.where(cfg == 0, mod_v[2:3, :wide], mod_v[2:3, width - wide:])
    for c in range(wide // LANES):
        part = slice(c * LANES, (c + 1) * LANES)
        put(gate, jnp.where(is_text, gate_text[:, part], gate_video[:, part]).T, c)
        for g in range(GROUPS):
            put(wo_turned.at[g], wo_buf[g * cols:(g + 1) * cols, part].T, c)

    landed(place_in, n - 1, p_r)
    lane = lax.broadcasted_iota(jnp.int32, (rows, LANES), 1)
    sub = lax.broadcasted_iota(jnp.int32, (rows, LANES), 0)

    def masked(j):
        at = place_in[j] * rows + sub
        return jnp.where(jnp.logical_or(at >= TXT, at < count), 0.0, MASKED)

    for p in range(steps):
        even, odd = masked(2 * p), masked(2 * p + 1)
        keys[p * rows:(p + 1) * rows, LANES:] = jnp.where(
            lane == 0, even, jnp.where(lane == 1, odd, 0.0)).astype(bf)
    values[HEAD:] = jnp.ones((values.shape[0] - HEAD, n * rows), bf)

    landed(kv_in, n - 1, kv_r)
    for p in range(steps):
        both = jnp.concatenate([kv_in[2 * p, :HEAD], kv_in[2 * p + 1, :HEAD]], axis=0)
        keys[p * rows:(p + 1) * rows, :LANES] = both.T
        values[:HEAD, p * rows:(p + 1) * rows] = kv_in[2 * p, HEAD:]
        values[:HEAD, span + p * rows:span + (p + 1) * rows] = kv_in[2 * p + 1, HEAD:]

    chip = lax.div(me, 2)

    def chip_of(k):
        mask = jnp.where(k == 0, 1, jnp.where(k <= 4, k + 3, jnp.where(k <= 6, k - 3, 0)))
        c0, c1, c2 = lax.rem(chip, 2), lax.rem(lax.div(chip, 2), 2), lax.div(chip, 4)
        k0, k1, k2 = lax.rem(mask, 2), lax.rem(lax.div(mask, 2), 2), lax.div(mask, 4)
        return 4 * flip(c2, k2) + 2 * flip(c1, k1) + flip(c0, k0)

    own_weight = jnp.where(cfg == 0, GUIDANCE, 1.0 - GUIDANCE)
    far_weight = 1.0 - own_weight

    def give(k):
        pair = chip_of(k)
        base = 2 * pair
        part = att_far.at[pl.ds(base, 2)]
        pltpu.make_async_copy(part, part, x_r.at[pair]).wait()
        for i in range(2):
            blend = own_weight * att_own[base + i].astype(f32) + far_weight * att_far[base + i].astype(f32)
            mixed[base + i] = blend.astype(bf)
            send(mixed, att_in, base + i, a_s, a_r.at[plane])

    row = lax.broadcasted_iota(jnp.int32, (LANES, 2 * rows), 0)
    first_row = jnp.where(row == 0, 1.0, 0.0).astype(bf)
    second_row = jnp.where(row == 1, 1.0, 0.0).astype(bf)
    blank = jnp.zeros((HEAD, 2 * rows), bf)

    def attend(k, carry):
        pair = chip_of(k)
        base = 2 * pair
        for i in range(2):
            @pl.when(base + i != me)
            def _():
                pltpu.make_async_copy(q_in.at[base + i], q_in.at[base + i], q_r.at[base + i]).wait()
        query = jnp.concatenate([q_in[base], q_in[base + 1]], axis=1)
        upper = jnp.concatenate([query, blank, first_row], axis=0)
        lower = jnp.concatenate([blank, query, second_row], axis=0)
        even = jnp.dot(keys[...], upper, preferred_element_type=f32)
        odd = jnp.dot(keys[...], lower, preferred_element_type=f32)
        highest = jnp.maximum(jnp.max(even, axis=0, keepdims=True), jnp.max(odd, axis=0, keepdims=True))
        numer = jnp.dot(values[:, :span], jnp.exp(even - highest).astype(bf), preferred_element_type=f32)
        numer += jnp.dot(values[:, span:], jnp.exp(odd - highest).astype(bf), preferred_element_type=f32)
        result = (numer[:HEAD] / numer[HEAD:HEAD + 1]).astype(bf)
        att_own[base] = result[:, :rows]
        att_own[base + 1] = result[:, rows:]
        pltpu.make_async_remote_copy(
            src_ref=att_own.at[pl.ds(base, 2)], dst_ref=att_far.at[pl.ds(base, 2)],
            send_sem=x_s, recv_sem=x_r.at[pair],
            device_id={"cfg": 1 - cfg}, device_id_type=MESH).start()

        @pl.when(k >= 2)
        def _():
            give(k - 2)

        return carry

    lax.fori_loop(0, steps, attend, 0)
    give(steps - 2)
    give(steps - 1)

    total = None
    for i in (3, 2, 0, 1):
        g = group(i)
        landed(att_in, heads_here - 1 if i == 3 else heads_here, a_r.at[g])
        part = att_in[pl.ds(g * heads_here, heads_here)].reshape(cols, rows)
        term = jnp.dot(wo_turned[g], part, preferred_element_type=f32)
        total = term if total is None else total + term
    out_ref[...] = gate[...] * total

    landed(kv_out, n - 1, kv_s)
    landed(q_out, n - 1, q_s)
    landed(place_in, n - 1, p_s)
    landed(att_own, n, x_s)
    landed(mixed, n - 1, a_s)


def whole_kernel(hidden, modulation, w_qkv, q_gain, k_gain, w_out, text_count, block_order):
    n = lax.axis_size("seq")
    states = hidden[0]
    rows, width = states.shape
    features = w_out.shape[0]
    cols = features // GROUPS
    half = width // 2
    wide = -(-half // LANES) * LANES
    bf, f32 = jnp.bfloat16, jnp.float32
    hbm = pl.BlockSpec(memory_space=pltpu.HBM)
    dma = pltpu.SemaphoreType.DMA
    turned = pl.pallas_call(
        functools.partial(fused, n),
        out_shape=jax.ShapeDtypeStruct((half, rows), f32),
        in_specs=[hbm] * 8,
        out_specs=pl.BlockSpec(memory_space=pltpu.VMEM),
        scratch_shapes=[
            pltpu.VMEM((1, 1), jnp.int32),
            pltpu.VMEM((1, 1), jnp.int32),
            pltpu.VMEM((rows, width), bf),
            pltpu.VMEM(modulation.shape, f32),
            pltpu.VMEM((1, HEAD), f32),
            pltpu.VMEM((1, HEAD), f32),
            pltpu.VMEM((3, GROUPS, width, cols), bf),
            pltpu.VMEM((features, wide), bf),
            pltpu.VMEM((GROUPS, half, cols), bf),
            pltpu.VMEM((half, rows), f32),
            pltpu.VMEM((rows, width), bf),
            pltpu.VMEM((n, 2 * HEAD, rows), bf),
            pltpu.VMEM((n, 2 * HEAD, rows), bf),
            pltpu.VMEM((n, HEAD, rows), bf),
            pltpu.VMEM((n, HEAD, rows), bf),
            pltpu.VMEM((1, 1, LANES), jnp.int32),
            pltpu.VMEM((n, 1, LANES), jnp.int32),
            pltpu.VMEM((n * rows // 2, 2 * LANES), bf),
            pltpu.VMEM((HEAD + 16, n * rows), bf),
        ] + [pltpu.VMEM((n, HEAD, rows), bf)] * 4 + [
            dma((6,)), dma((3, GROUPS)), dma,
            dma, dma, dma, dma((n,)), dma, dma, dma, dma((n // 2,)), dma, dma((GROUPS,)),
        ],
        compiler_params=pltpu.CompilerParams(
            collective_id=0, has_side_effects=True, vmem_limit_bytes=40 * 1024 * 1024),
    )(text_count[None], block_order[None], states, modulation, w_qkv, q_gain[None], k_gain[None], w_out)
    return turned.T


def solution(mesh):
    in_specs = (P("cfg", "seq", None), P(), P(), P(), P(), P(), P("cfg"), P("seq"))
    out_specs = P("seq", "cfg")
    one_head_each = mesh.shape["seq"] == HEADS and mesh.shape["cfg"] == 2
    body = whole_kernel if one_head_each else shards
    return jax.shard_map(body, mesh=mesh, in_specs=in_specs, out_specs=out_specs, check_vma=False)
```

time: 50.2 us -> 47.8 us (0.952)
  Pallas kernels: 45.3 us -> 40.2 us
  local copies, waits for them, and re-layouts: 2.02 us -> 6.05 us
  other arithmetic: 1.32 us -> 0 us
    unnamed x0 -> x11, local copies, waits for them, and re-layouts: none -> 6.05 us
    pallas_call x1, Pallas kernels: 45.3 us -> 40.2 us  [whole_kernel(): pl.pallas_call(functools.partial(fused, n), out_shape=jax.ShapeDtypeStruc...]
    pallas_call x1 -> x0, local copies, waits for them, and re-layouts: 2.02 us -> none  [whole_kernel(): pl.pallas_call(functools.partial(fused, n), out_shape=jax.ShapeDtypeStruc...]
    broadcast_in_dim x1 -> x0, other arithmetic: 1.32 us -> none  [whole_kernel(): double = lambda gain: jnp.concatenate([gain, gain])[None, :]]
where the time goes in v1:
time: 47.8 us; the launch traced here: 47.6 us
  Pallas kernels  40.2 us (84%)
  local copies, waits for them, and re-layouts  6.05 us (13%)
  between operations  1.32 us (3%)
    pallas_call x1, Pallas kernels, whole_kernel(): pl.pallas_call(functools.partial(fused, n), out_shape=jax.ShapeDtypeStruc...  40.2 us
    unnamed x11, local copies, waits for them, and re-layouts  6.05 us

profile of v1, /device:TPU:0, one launch (start us, length us, event | category | flops | bytes accessed | tf_op | source)
XLA Modules:
  0.0 47.6 jit_solution(422349458619149490)
XLA Ops:
  1.3 0.0 copy-start
  1.3 2.1 %copy-done = bf16[1024,1920]{1,0:T(8,128)(2,1)S(1)} copy-done((bf16[1024,1920]{1,0:T(8,128)(2,1)S(1)}, bf16[1024,1920]{1,0:T(8,128)(2,1)}, u32[]{:S(2)}) %copy-start) | copy-done | bytes 3932184
  3.4 0.0 copy-start.1
  3.4 1.0 %copy-done.1 = bf16[1,128,1920]{2,1,0:T(8,128)(2,1)S(1)} copy-done((bf16[1,128,1920]{2,1,0:T(8,128)(2,1)S(1)}, bf16[1,128,1920]{2,1,0:T(8,128)(2,1)}, u32[]{:S(2)}) %copy-start.1) | copy-done | bytes 491544
  4.4 0.0 copy-start.2
  4.4 0.8 %copy-done.2 = f32[6,1920]{1,0:T(8,128)S(1)} copy-done((f32[6,1920]{1,0:T(8,128)S(1)}, f32[6,1920]{1,0:T(8,128)}, u32[]{:S(2)}) %copy-start.2) | copy-done | bytes 46104
  5.3 0.0 copy-start.3
  5.3 0.7 %copy-done.3 = f32[64]{0:T(128)S(1)} copy-done((f32[64]{0:T(128)S(1)}, f32[64]{0:T(128)}, u32[]{:S(2)}) %copy-start.3) | copy-done | bytes 280
  5.9 0.0 copy-start.4
  5.9 0.7 %copy-done.4 = f32[64]{0:T(128)S(1)} copy-done((f32[64]{0:T(128)S(1)}, f32[64]{0:T(128)}, u32[]{:S(2)}) %copy-start.4) | copy-done | bytes 280
  6.6 40.2 %shard_map.82 = f32[960,128]{1,0:T(8,128)S(1)} custom-call(s32[1,1]{1,0:T(1,128)} %bitcast.6.count_ref, s32[1,1]{1,0:T(1,128)} %bitcast.7.block_ref, bf16[128,1920]{1,0:T(8,128)(2,1)S(1)} %bitcast.9, f32[6,1920]{1,0:T(8,128)S(1)} %copy-done.2, bf16[3,1920,1024]{2,1,0:T(8,128)(2,1)} %w_ref.1, f32[1,64]{1,0:T(1,128)S(1)} %bitcast.10, f32[1,64]{1,0:T(1,128)S(1)} %bitcast.11, ...), custom_call_target="tpu_custom_call" | custom-call | tf_op jit(solution)/shard_map/pallas_call | solution.py:395
  46.8 0.8 %copy.12 = f32[128,960]{0,1:T(8,128)} copy(f32[128,960]{0,1:T(8,128)S(1)} %bitcast.8) | data formatting | bytes 983040
Async XLA Ops:
  1.3 2.1 %copy-start = (bf16[1024,1920]{1,0:T(8,128)(2,1)S(1)}, bf16[1024,1920]{1,0:T(8,128)(2,1)}, u32[]{:S(2)}) copy-start(bf16[1024,1920]{1,0:T(8,128)(2,1)} %wo_ref.1) | copy-start | bytes 11796484
  3.4 1.0 %copy-start.1 = (bf16[1,128,1920]{2,1,0:T(8,128)(2,1)S(1)}, bf16[1,128,1920]{2,1,0:T(8,128)(2,1)}, u32[]{:S(2)}) copy-start(bf16[1,128,1920]{2,1,0:T(8,128)(2,1)} %param.8) | copy-start | bytes 1474564
  4.4 0.8 %copy-start.2 = (f32[6,1920]{1,0:T(8,128)S(1)}, f32[6,1920]{1,0:T(8,128)}, u32[]{:S(2)}) copy-start(f32[6,1920]{1,0:T(8,128)} %mod_ref.1) | copy-start | bytes 138244
  5.3 0.7 %copy-start.3 = (f32[64]{0:T(128)S(1)}, f32[64]{0:T(128)}, u32[]{:S(2)}) copy-start(f32[64]{0:T(128)} %param.11) | copy-start | bytes 772
  5.9 0.7 %copy-start.4 = (f32[64]{0:T(128)S(1)}, f32[64]{0:T(128)}, u32[]{:S(2)}) copy-start(f32[64]{0:T(128)} %param.12) | copy-start | bytes 772

commit v2 on v1

--- a/solution.py
+++ b/solution.py
@@ -115,6 +115,7 @@
 
 LANES = 128
 GROUPS = 4
+SHIFT = 256
 MESH = pl.DeviceIdType.MESH
 
 
@@ -128,8 +129,8 @@
     return centred * lax.rsqrt(spread + EPSILON)
 
 
-def fused(n, count_ref, block_ref, hidden_ref, mod_ref, w_ref, qg_ref, kg_ref, wo_ref, out_ref,
-          count_v, block_v, hidden_v, mod_v, qg_v, kg_v, w_buf, wo_buf, wo_turned, gate, modded,
+def fused(n, info_ref, hidden_ref, mod_ref, w_ref, qg_ref, kg_ref, wo_ref, out_ref,
+          hidden_v, mod_v, qg_v, kg_v, w_buf, wo_buf, wo_turned, gate, modded,
           kv_out, kv_in, q_out, q_in, place_out, place_in, keys, values,
           att_own, att_far, mixed, att_in,
           in_sem, w_sem, wo_sem, kv_s, kv_r, q_s, q_r, p_s, p_r, x_s, x_r, a_s, a_r):
@@ -169,7 +170,7 @@
     column = pl.multiple_of(cfg * (width - wide), LANES)
     out_weight = pltpu.make_async_copy(wo_ref.at[:, pl.ds(column, wide)], wo_buf, wo_sem)
     inputs = [pltpu.make_async_copy(a, b, in_sem.at[i]) for i, (a, b) in enumerate([
-        (hidden_ref, hidden_v), (mod_ref, mod_v), (block_ref, block_v), (count_ref, count_v),
+        (hidden_ref, hidden_v), (mod_ref, mod_v),
         (kg_ref, kg_v), (qg_ref, qg_v)])]
     for copy in inputs:
         copy.start()
@@ -193,8 +194,8 @@
 
     for copy in inputs:
         copy.wait()
-    block = block_v[...]
-    count = count_v[...]
+    block = lax.div(info_ref[0], SHIFT)
+    count = lax.rem(info_ref[0], SHIFT)
     mod = mod_v[...]
     down = block * rows + lax.broadcasted_iota(jnp.int32, (rows, 1), 0)
     is_text = down < TXT
@@ -216,8 +217,8 @@
 
     k_gain = down_lanes(kg_v[...])
     q_gain = down_lanes(qg_v[...]) * HEAD ** (-0.5)
-    place_out[0] = jnp.broadcast_to(block, (1, LANES))
-    place_in[me] = jnp.broadcast_to(block, (1, LANES))
+    place_out[0] = jnp.full((1, LANES), block, jnp.int32)
+    place_in[me] = jnp.full((1, LANES), block, jnp.int32)
 
     def project_kv(i):
         weight(1, i).wait()
@@ -395,11 +396,9 @@
     turned = pl.pallas_call(
         functools.partial(fused, n),
         out_shape=jax.ShapeDtypeStruct((half, rows), f32),
-        in_specs=[hbm] * 8,
+        in_specs=[pl.BlockSpec(memory_space=pltpu.SMEM)] + [hbm] * 6,
         out_specs=pl.BlockSpec(memory_space=pltpu.VMEM),
         scratch_shapes=[
-            pltpu.VMEM((1, 1), jnp.int32),
-            pltpu.VMEM((1, 1), jnp.int32),
             pltpu.VMEM((rows, width), bf),
             pltpu.VMEM(modulation.shape, f32),
             pltpu.VMEM((1, HEAD), f32),
@@ -418,12 +417,13 @@
             pltpu.VMEM((n * rows // 2, 2 * LANES), bf),
             pltpu.VMEM((HEAD + 16, n * rows), bf),
         ] + [pltpu.VMEM((n, HEAD, rows), bf)] * 4 + [
-            dma((6,)), dma((3, GROUPS)), dma,
+            dma((4,)), dma((3, GROUPS)), dma,
             dma, dma, dma, dma((n,)), dma, dma, dma, dma((n // 2,)), dma, dma((GROUPS,)),
         ],
         compiler_params=pltpu.CompilerParams(
             collective_id=0, has_side_effects=True, vmem_limit_bytes=40 * 1024 * 1024),
-    )(text_count[None], block_order[None], states, modulation, w_qkv, q_gain[None], k_gain[None], w_out)
+    )(block_order * SHIFT + text_count, *[pltpu.with_memory_space_constraint(x, pltpu.HBM) for x in (
+        states, modulation, w_qkv, q_gain[None], k_gain[None], w_out)])
     return turned.T
 
 

time: 47.8 us -> 42.5 us (0.89)
  local copies, waits for them, and re-layouts: 6.05 us -> 0.78 us
    unnamed x11 -> x1, local copies, waits for them, and re-layouts: 6.05 us -> 0.78 us
where the time goes in v2:
time: 42.5 us; the launch traced here: 42.4 us
  Pallas kernels  40.3 us (95%)
  between operations  1.31 us (3%)
  local copies, waits for them, and re-layouts  0.78 us (2%)
    pallas_call x1, Pallas kernels, whole_kernel(): pl.pallas_call(functools.partial(fused, n), out_shape=jax.ShapeDtypeStruc...  40.3 us

profile of v2, /device:TPU:0, one launch (start us, length us, event | category | flops | bytes accessed | tf_op | source)
XLA Modules:
  0.0 42.4 jit_solution(5900223986148676795)
XLA Ops:
  1.3 40.3 %shard_map.82 = f32[960,128]{1,0:T(8,128)S(1)} custom-call(s32[1]{0:T(128)S(6)} %add.3.info_ref, bf16[128,1920]{1,0:T(8,128)(2,1)} %bitcast.5, f32[6,1920]{1,0:T(8,128)} %mod_ref.1, bf16[3,1920,1024]{2,1,0:T(8,128)(2,1)} %w_ref.1, f32[1,64]{1,0:T(1,128)} %bitcast.6, f32[1,64]{1,0:T(1,128)} %bitcast.7, bf16[1024,1920]{1,0:T(8,128)(2,1)} %wo_ref.1), custom_call_target="tpu_custom_call" | custom-call | tf_op jit(solution)/shard_map/pallas_call | solution.py:396
  41.6 0.8 %copy.12 = f32[128,960]{0,1:T(8,128)} copy(f32[128,960]{0,1:T(8,128)S(1)} %bitcast.4) | data formatting | bytes 983040

commit v3 on v2

--- a/solution.py
+++ b/solution.py
@@ -132,7 +132,7 @@
 def fused(n, info_ref, hidden_ref, mod_ref, w_ref, qg_ref, kg_ref, wo_ref, out_ref,
           hidden_v, mod_v, qg_v, kg_v, w_buf, wo_buf, wo_turned, gate, modded,
           kv_out, kv_in, q_out, q_in, place_out, place_in, keys, values,
-          att_own, att_far, mixed, att_in,
+          att_own, att_far, mixed, att_in, held_a, held_b,
           in_sem, w_sem, wo_sem, kv_s, kv_r, q_s, q_r, p_s, p_r, x_s, x_r, a_s, a_r):
     me = lax.axis_index("seq")
     cfg = lax.axis_index("cfg")
@@ -154,10 +154,11 @@
         pl.semaphore_signal(barrier, inc=1, device_id={"seq": lax.rem(me + j, n)}, device_id_type=MESH)
     pl.semaphore_signal(barrier, inc=1, device_id={"cfg": 1 - cfg}, device_id_type=MESH)
 
+    outer = plane_high == plane_low
+
     def group(i):
-        high = 1 - lax.div(i, 2)
-        lowbit = flip(lax.div(i, 2), lax.rem(i, 2))
-        return 2 * flip(plane_high, high) + flip(plane_low, lowbit)
+        mask = jnp.where(outer, lax.rem(i + 1, GROUPS), jnp.where(i == 3, 0, lax.rem(i + 1, 3) + 1))
+        return 2 * flip(plane_high, lax.div(mask, 2)) + flip(plane_low, lax.rem(mask, 2))
 
     def member(first, h):
         return first + 2 * flip(side, h // 2) + flip(core, h % 2)
@@ -233,37 +234,38 @@
             kv_out[first + h, HEAD:] = v_all[part].astype(bf)
 
     def send_kv(i):
-        first = group(i) * heads_here
+        if isinstance(i, int):
+            pl.semaphore_wait(barrier, n)
+            for j in range(1, n):
+                pltpu.make_async_remote_copy(
+                    src_ref=place_out.at[0], dst_ref=place_in.at[me], send_sem=p_s, recv_sem=p_r,
+                    device_id={"seq": lax.rem(me + j, n)}, device_id_type=MESH).start()
         for h in range(heads_here):
-            send(kv_out, kv_in, member(first, h), kv_s, kv_r)
-
-    project_kv(0)
-    pl.semaphore_wait(barrier, n)
-    send_kv(0)
-    for j in range(1, n):
-        pltpu.make_async_remote_copy(
-            src_ref=place_out.at[0], dst_ref=place_in.at[me], send_sem=p_s, recv_sem=p_r,
-            device_id={"seq": lax.rem(me + j, n)}, device_id_type=MESH).start()
+            send(kv_out, kv_in, member(group(i) * heads_here, h), kv_s, kv_r)
 
     def rest_kv(i, carry):
         project_kv(i)
         send_kv(i)
         return carry
 
+    project_kv(0)
+    send_kv(0)
     lax.fori_loop(1, GROUPS, rest_kv, 0)
 
-    def project_q(i, carry):
+    def project_q(i):
         weight(0, i).wait()
         first = group(i) * heads_here
         q_all = jnp.dot(modded[...], w_buf[0, i], preferred_element_type=f32).T
         for h in range(heads_here):
             part = slice(h * HEAD, (h + 1) * HEAD)
             q_out[first + h] = (column_normal(q_all[part]) * q_gain).astype(bf)
+
+    def send_q(i):
         for h in range(heads_here):
-            send(q_out, q_in, member(first, h), q_s, q_r.at[me])
-        return carry
-
-    lax.fori_loop(0, GROUPS, project_q, 0)
+            send(q_out, q_in, member(group(i) * heads_here, h), q_s, q_r.at[me])
+
+    lax.fori_loop(0, GROUPS, lambda i, carry: (project_q(i), carry)[1], 0)
+    send_q(3)
 
     out_weight.wait()
 
@@ -300,7 +302,18 @@
             lane == 0, even, jnp.where(lane == 1, odd, 0.0)).astype(bf)
     values[HEAD:] = jnp.ones((values.shape[0] - HEAD, n * rows), bf)
 
-    landed(kv_in, n - 1, kv_r)
+    @pl.when(outer)
+    def _():
+        landed(kv_in, n - 1, kv_r)
+
+    landed(kv_out, n - 1, kv_s)
+    for i in range(3):
+        send_q(i)
+
+    @pl.when(jnp.logical_not(outer))
+    def _():
+        landed(kv_in, n - 1, kv_r)
+
     for p in range(steps):
         both = jnp.concatenate([kv_in[2 * p, :HEAD], kv_in[2 * p + 1, :HEAD]], axis=0)
         keys[p * rows:(p + 1) * rows, :LANES] = both.T
@@ -310,7 +323,7 @@
     chip = lax.div(me, 2)
 
     def chip_of(k):
-        mask = jnp.where(k == 0, 1, jnp.where(k <= 4, k + 3, jnp.where(k <= 6, k - 3, 0)))
+        mask = jnp.where(k <= 1, 1 - k, jnp.where(k >= 5, k, jnp.where(k == 3, 4, lax.div(k, 2) + 1)))
         c0, c1, c2 = lax.rem(chip, 2), lax.rem(lax.div(chip, 2), 2), lax.div(chip, 4)
         k0, k1, k2 = lax.rem(mask, 2), lax.rem(lax.div(mask, 2), 2), lax.div(mask, 4)
         return 4 * flip(c2, k2) + 2 * flip(c1, k1) + flip(c0, k0)
@@ -333,11 +346,10 @@
     second_row = jnp.where(row == 1, 1.0, 0.0).astype(bf)
     blank = jnp.zeros((HEAD, 2 * rows), bf)
 
-    def attend(k, carry):
-        pair = chip_of(k)
-        base = 2 * pair
+    def score(k, held):
+        base = 2 * chip_of(jnp.minimum(k, steps - 1))
         for i in range(2):
-            @pl.when(base + i != me)
+            @pl.when(jnp.logical_and(base + i != me, k < steps))
             def _():
                 pltpu.make_async_copy(q_in.at[base + i], q_in.at[base + i], q_r.at[base + i]).wait()
         query = jnp.concatenate([q_in[base], q_in[base + 1]], axis=1)
@@ -345,9 +357,18 @@
         lower = jnp.concatenate([blank, query, second_row], axis=0)
         even = jnp.dot(keys[...], upper, preferred_element_type=f32)
         odd = jnp.dot(keys[...], lower, preferred_element_type=f32)
-        highest = jnp.maximum(jnp.max(even, axis=0, keepdims=True), jnp.max(odd, axis=0, keepdims=True))
-        numer = jnp.dot(values[:, :span], jnp.exp(even - highest).astype(bf), preferred_element_type=f32)
-        numer += jnp.dot(values[:, span:], jnp.exp(odd - highest).astype(bf), preferred_element_type=f32)
+        held[:span] = even
+        held[span:] = odd
+        return jnp.maximum(jnp.max(even, axis=0, keepdims=True), jnp.max(odd, axis=0, keepdims=True))
+
+    def weigh(k, held, highest):
+        pair = chip_of(k)
+        base = 2 * pair
+        numer = None
+        for c in range(0, n * rows, 2 * rows):
+            part = jnp.exp(held[c:c + 2 * rows] - highest).astype(bf)
+            term = jnp.dot(values[:, c:c + 2 * rows], part, preferred_element_type=f32)
+            numer = term if numer is None else numer + term
         result = (numer[:HEAD] / numer[HEAD:HEAD + 1]).astype(bf)
         att_own[base] = result[:, :rows]
         att_own[base + 1] = result[:, rows:]
@@ -356,26 +377,37 @@
             send_sem=x_s, recv_sem=x_r.at[pair],
             device_id={"cfg": 1 - cfg}, device_id_type=MESH).start()
 
-        @pl.when(k >= 2)
-        def _():
-            give(k - 2)
-
-        return carry
-
-    lax.fori_loop(0, steps, attend, 0)
-    give(steps - 2)
-    give(steps - 1)
-
+    lag = 4
+
+    def attend(i, highest):
+        for part in range(2):
+            k = 2 * i + part
+            held, later = (held_a, held_b) if part == 0 else (held_b, held_a)
+            following = score(k + 1, later)
+            weigh(k, held, highest)
+            highest = following
+
+            @pl.when(k >= lag)
+            def _():
+                give(k - lag)
+
+        return highest
+
+    lax.fori_loop(0, steps // 2, attend, score(0, held_a))
+    for k in range(steps - lag, steps):
+        give(k)
+
+    near = jnp.where(outer, 0, 2)
+    order = (3, near, lax.rem(near + 1, 3), lax.rem(near + 2, 3))
     total = None
-    for i in (3, 2, 0, 1):
+    for i in order:
         g = group(i)
-        landed(att_in, heads_here - 1 if i == 3 else heads_here, a_r.at[g])
+        landed(att_in, heads_here - 1 if i is order[0] else heads_here, a_r.at[g])
         part = att_in[pl.ds(g * heads_here, heads_here)].reshape(cols, rows)
         term = jnp.dot(wo_turned[g], part, preferred_element_type=f32)
         total = term if total is None else total + term
     out_ref[...] = gate[...] * total
 
-    landed(kv_out, n - 1, kv_s)
     landed(q_out, n - 1, q_s)
     landed(place_in, n - 1, p_s)
     landed(att_own, n, x_s)
@@ -416,7 +448,7 @@
             pltpu.VMEM((n, 1, LANES), jnp.int32),
             pltpu.VMEM((n * rows // 2, 2 * LANES), bf),
             pltpu.VMEM((HEAD + 16, n * rows), bf),
-        ] + [pltpu.VMEM((n, HEAD, rows), bf)] * 4 + [
+        ] + [pltpu.VMEM((n, HEAD, rows), bf)] * 4 + [pltpu.VMEM((n * rows, 2 * rows), f32)] * 2 + [
             dma((4,)), dma((3, GROUPS)), dma,
             dma, dma, dma, dma((n,)), dma, dma, dma, dma((n // 2,)), dma, dma((GROUPS,)),
         ],

time: 42.5 us -> 37.1 us (0.87)
  Pallas kernels: 40.3 us -> 34.9 us
    pallas_call x1, Pallas kernels: 40.3 us -> 34.9 us  [whole_kernel(): pl.pallas_call(functools.partial(fused, n), out_shape=jax.ShapeDtypeStruc...]
where the time goes in v3:
time: 37.1 us; the launch traced here: 37 us
  Pallas kernels  34.9 us (94%)
  between operations  1.31 us (4%)
  local copies, waits for them, and re-layouts  0.78 us (2%)
    pallas_call x1, Pallas kernels, whole_kernel(): pl.pallas_call(functools.partial(fused, n), out_shape=jax.ShapeDtypeStruc...  34.9 us
    unnamed x1, local copies, waits for them, and re-layouts  0.78 us

profile of v3, /device:TPU:0, one launch (start us, length us, event | category | flops | bytes accessed | tf_op | source)
XLA Modules:
  0.0 37.0 jit_solution(11875243772871914112)
XLA Ops:
  1.3 34.9 %shard_map.82 = f32[960,128]{1,0:T(8,128)S(1)} custom-call(s32[1]{0:T(128)S(6)} %add.3.info_ref, bf16[128,1920]{1,0:T(8,128)(2,1)} %bitcast.5, f32[6,1920]{1,0:T(8,128)} %mod_ref.1, bf16[3,1920,1024]{2,1,0:T(8,128)(2,1)} %w_ref.1, f32[1,64]{1,0:T(1,128)} %bitcast.6, f32[1,64]{1,0:T(1,128)} %bitcast.7, bf16[1024,1920]{1,0:T(8,128)(2,1)} %wo_ref.1), custom_call_target="tpu_custom_call" | custom-call | tf_op jit(solution)/shard_map/pallas_call | solution.py:428
  36.2 0.8 %copy.12 = f32[128,960]{0,1:T(8,128)} copy(f32[128,960]{0,1:T(8,128)S(1)} %bitcast.4) | data formatting | bytes 983040

commit v4 on v3

--- a/solution.py
+++ b/solution.py
@@ -116,6 +116,7 @@
 LANES = 128
 GROUPS = 4
 SHIFT = 256
+ORDER = (1, 0, 2, 4, 3, 5, 6, 7)
 MESH = pl.DeviceIdType.MESH
 
 
@@ -156,9 +157,12 @@
 
     outer = plane_high == plane_low
 
+    def plane_at(mask):
+        return 2 * flip(plane_high, mask // 2) + flip(plane_low, mask % 2)
+
     def group(i):
         mask = jnp.where(outer, lax.rem(i + 1, GROUPS), jnp.where(i == 3, 0, lax.rem(i + 1, 3) + 1))
-        return 2 * flip(plane_high, lax.div(mask, 2)) + flip(plane_low, lax.rem(mask, 2))
+        return plane_at(mask)
 
     def member(first, h):
         return first + 2 * flip(side, h // 2) + flip(core, h % 2)
@@ -260,12 +264,12 @@
             part = slice(h * HEAD, (h + 1) * HEAD)
             q_out[first + h] = (column_normal(q_all[part]) * q_gain).astype(bf)
 
-    def send_q(i):
+    def send_q(mask):
         for h in range(heads_here):
-            send(q_out, q_in, member(group(i) * heads_here, h), q_s, q_r.at[me])
+            send(q_out, q_in, member(plane_at(mask) * heads_here, h), q_s.at[mask], q_r.at[me])
 
     lax.fori_loop(0, GROUPS, lambda i, carry: (project_q(i), carry)[1], 0)
-    send_q(3)
+    send_q(0)
 
     out_weight.wait()
 
@@ -307,8 +311,9 @@
         landed(kv_in, n - 1, kv_r)
 
     landed(kv_out, n - 1, kv_s)
-    for i in range(3):
-        send_q(i)
+    send_q(1)
+    send_q(2)
+    send_q(3)
 
     @pl.when(jnp.logical_not(outer))
     def _():
@@ -323,7 +328,7 @@
     chip = lax.div(me, 2)
 
     def chip_of(k):
-        mask = jnp.where(k <= 1, 1 - k, jnp.where(k >= 5, k, jnp.where(k == 3, 4, lax.div(k, 2) + 1)))
+        mask = sum(jnp.where(k == i, at, 0) for i, at in enumerate(ORDER))
         c0, c1, c2 = lax.rem(chip, 2), lax.rem(lax.div(chip, 2), 2), lax.div(chip, 4)
         k0, k1, k2 = lax.rem(mask, 2), lax.rem(lax.div(mask, 2), 2), lax.div(mask, 4)
         return 4 * flip(c2, k2) + 2 * flip(c1, k1) + flip(c0, k0)
@@ -347,9 +352,9 @@
     blank = jnp.zeros((HEAD, 2 * rows), bf)
 
     def score(k, held):
-        base = 2 * chip_of(jnp.minimum(k, steps - 1))
+        base = 2 * chip_of(k)
         for i in range(2):
-            @pl.when(jnp.logical_and(base + i != me, k < steps))
+            @pl.when(base + i != me)
             def _():
                 pltpu.make_async_copy(q_in.at[base + i], q_in.at[base + i], q_r.at[base + i]).wait()
         query = jnp.concatenate([q_in[base], q_in[base + 1]], axis=1)
@@ -377,7 +382,12 @@
             send_sem=x_s, recv_sem=x_r.at[pair],
             device_id={"cfg": 1 - cfg}, device_id_type=MESH).start()
 
-    lag = 4
+    lag = 3
+
+    def late_gift(k):
+        @pl.when(k >= lag)
+        def _():
+            give(k - lag)
 
     def attend(i, highest):
         for part in range(2):
@@ -386,32 +396,32 @@
             following = score(k + 1, later)
             weigh(k, held, highest)
             highest = following
-
-            @pl.when(k >= lag)
-            def _():
-                give(k - lag)
-
+            late_gift(k)
         return highest
 
-    lax.fori_loop(0, steps // 2, attend, score(0, held_a))
+    highest = lax.fori_loop(0, steps // 2 - 1, attend, score(0, held_a))
+    following = score(steps - 1, held_b)
+    weigh(steps - 2, held_a, highest)
+    give(steps - 2 - lag)
+    weigh(steps - 1, held_b, following)
+    give(steps - 1 - lag)
     for k in range(steps - lag, steps):
         give(k)
 
-    near = jnp.where(outer, 0, 2)
-    order = (3, near, lax.rem(near + 1, 3), lax.rem(near + 2, 3))
+    for mask in range(GROUPS):
+        landed(q_out, heads_here if mask else heads_here - 1, q_s.at[mask])
+    landed(place_in, n - 1, p_s)
+    landed(att_own, n, x_s)
+    landed(mixed, n - 1, a_s)
+
     total = None
-    for i in order:
-        g = group(i)
-        landed(att_in, heads_here - 1 if i is order[0] else heads_here, a_r.at[g])
+    for mask in (0, 1, 2, 3):
+        g = plane_at(mask)
+        landed(att_in, heads_here if mask else heads_here - 1, a_r.at[g])
         part = att_in[pl.ds(g * heads_here, heads_here)].reshape(cols, rows)
         term = jnp.dot(wo_turned[g], part, preferred_element_type=f32)
         total = term if total is None else total + term
     out_ref[...] = gate[...] * total
-
-    landed(q_out, n - 1, q_s)
-    landed(place_in, n - 1, p_s)
-    landed(att_own, n, x_s)
-    landed(mixed, n - 1, a_s)
 
 
 def whole_kernel(hidden, modulation, w_qkv, q_gain, k_gain, w_out, text_count, block_order):
@@ -450,7 +460,7 @@
             pltpu.VMEM((HEAD + 16, n * rows), bf),
         ] + [pltpu.VMEM((n, HEAD, rows), bf)] * 4 + [pltpu.VMEM((n * rows, 2 * rows), f32)] * 2 + [
             dma((4,)), dma((3, GROUPS)), dma,
-            dma, dma, dma, dma((n,)), dma, dma, dma, dma((n // 2,)), dma, dma((GROUPS,)),
+            dma, dma, dma((GROUPS,)), dma((n,)), dma, dma, dma, dma((n // 2,)), dma, dma((GROUPS,)),
         ],
         compiler_params=pltpu.CompilerParams(
             collective_id=0, has_side_effects=True, vmem_limit_bytes=40 * 1024 * 1024),

time: 37.1 us -> 37 us (level)
  no operation moved by 1% of the time
where the time goes in v4:
time: 37 us; the launch traced here: 36.8 us
  Pallas kernels  34.7 us (94%)
  between operations  1.31 us (4%)
  local copies, waits for them, and re-layouts  0.78 us (2%)
    pallas_call x1, Pallas kernels, whole_kernel(): pl.pallas_call(functools.partial(fused, n), out_shape=jax.ShapeDtypeStruc...  34.7 us
    unnamed x1, local copies, waits for them, and re-layouts  0.78 us

profile of v4, /device:TPU:0, one launch (start us, length us, event | category | flops | bytes accessed | tf_op | source)
XLA Modules:
  0.0 36.8 jit_solution(2463310469032633922)
XLA Ops:
  1.3 34.7 %shard_map.82 = f32[960,128]{1,0:T(8,128)S(1)} custom-call(s32[1]{0:T(128)S(6)} %add.3.info_ref, bf16[128,1920]{1,0:T(8,128)(2,1)} %bitcast.5, f32[6,1920]{1,0:T(8,128)} %mod_ref.1, bf16[3,1920,1024]{2,1,0:T(8,128)(2,1)} %w_ref.1, f32[1,64]{1,0:T(1,128)} %bitcast.6, f32[1,64]{1,0:T(1,128)} %bitcast.7, bf16[1024,1920]{1,0:T(8,128)(2,1)} %wo_ref.1), custom_call_target="tpu_custom_call" | custom-call | tf_op jit(solution)/shard_map/pallas_call | solution.py:438
  36.0 0.8 %copy.12 = f32[128,960]{0,1:T(8,128)} copy(f32[128,960]{0,1:T(8,128)S(1)} %bitcast.4) | data formatting | bytes 983040

commit v5 on v4

--- a/solution.py
+++ b/solution.py
@@ -161,7 +161,7 @@
         return 2 * flip(plane_high, mask // 2) + flip(plane_low, mask % 2)
 
     def group(i):
-        mask = jnp.where(outer, lax.rem(i + 1, GROUPS), jnp.where(i == 3, 0, lax.rem(i + 1, 3) + 1))
+        mask = jnp.where(i == 3, 0, lax.rem(i + 1, 3) + 1)
         return plane_at(mask)
 
     def member(first, h):

time: 37 us -> 36.7 us (level)
  no operation moved by 1% of the time
where the time goes in v5:
time: 36.7 us; the launch traced here: 36.6 us
  Pallas kernels  34.5 us (94%)
  between operations  1.31 us (4%)
  local copies, waits for them, and re-layouts  0.78 us (2%)
    pallas_call x1, Pallas kernels, whole_kernel(): pl.pallas_call(functools.partial(fused, n), out_shape=jax.ShapeDtypeStruc...  34.5 us
    unnamed x1, local copies, waits for them, and re-layouts  0.78 us

profile of v5, /device:TPU:0, one launch (start us, length us, event | category | flops | bytes accessed | tf_op | source)
XLA Modules:
  0.0 36.6 jit_solution(11033367609470266203)
XLA Ops:
  1.3 34.5 %shard_map.82 = f32[960,128]{1,0:T(8,128)S(1)} custom-call(s32[1]{0:T(128)S(6)} %add.3.info_ref, bf16[128,1920]{1,0:T(8,128)(2,1)} %bitcast.5, f32[6,1920]{1,0:T(8,128)} %mod_ref.1, bf16[3,1920,1024]{2,1,0:T(8,128)(2,1)} %w_ref.1, f32[1,64]{1,0:T(1,128)} %bitcast.6, f32[1,64]{1,0:T(1,128)} %bitcast.7, bf16[1024,1920]{1,0:T(8,128)(2,1)} %wo_ref.1), custom_call_target="tpu_custom_call" | custom-call | tf_op jit(solution)/shard_map/pallas_call | solution.py:438
  35.8 0.8 %copy.12 = f32[128,960]{0,1:T(8,128)} copy(f32[128,960]{0,1:T(8,128)S(1)} %bitcast.4) | data formatting | bytes 983040
